TPU v7x, 256 devices: a whole 4x4x8 slice. The times are simulated.
256 devices in a mesh: row: 8 (over y, x_lo), col: 32 (over x_hi, z, core).
Axes of the slice: x: 4 (x_hi: 2, x_lo: 2; x = x_hi * 2 + x_lo), y: 4, z: 8, core: 2. Of those that a mesh axis runs over, the one named last changes fastest.
Arguments:
- inverse_state: float32 [4, 2048, 1, 8192], P(None, 'row', None, 'col')
- row_seeds: int32 [2, 4, 2048], P(None, None, 'row'), may hold values from 0 to 31
- col_seeds: int32 [2, 1, 8192], P(None, None, 'col'), may hold values from 0 to 31
Outputs:
- inverse: float32 [4, 2048, 1, 8192], P(None, 'row', None, 'col')
All inputs are finite; a program needn't handle non-finite values.
Results may differ from a plain program's by a relative error of at most 0.0002.
Values sent between devices are 32-bit elements; how exact they have to be, the bound alone decides.
No kernel may reach another device: no remote copies, remote signals or barrier semaphores. Data moves between devices by JAX's collectives and lax.ppermute only.
A program may use at most 64 MiB of HBM per device.

v0:
```python
import jax
import jax.numpy as jnp
from jax import lax
from jax.sharding import PartitionSpec as P

STEPS = 2
root_half = 0.7071067811865476


def filled_up(lines, length):
    spare = -len(lines) % length
    return jnp.pad(lines, [(0, spare)] + [(0, 0)] * (lines.ndim - 1))


def from_root(x, axis, root):
    lines = jnp.where(lax.axis_index(axis) == root, x, jnp.zeros_like(x)).reshape(
        -1, *x.shape[1:][-1:]
    )
    padded = filled_up(lines, lax.axis_size(axis))
    own = lax.psum_scatter(padded, axis, scatter_dimension=0, tiled=True)
    return lax.all_gather(own, axis, axis=0, tiled=True)[: len(lines)].reshape(x.shape)


def broadcast(x, axis, root):
    return lax.dynamic_index_in_dim(lax.all_gather(x, axis), root, 0, keepdims=False)


def swapped(block, axis, bit):
    count = lax.axis_size(axis)
    route = []
    for low in range(count):
        high = low | 1 << bit
        if high != low and high < count:
            route += [(low, high), (high, low)]
    return lax.ppermute(block, axis, route)


def seed_values(seeds):
    return (2.0 * seeds.astype(jnp.float32) - 31.0) / 16.0


def row_level(matrix, scales, groups):
    count = matrix.shape[0]
    half = count // (2 * groups)
    shaped = matrix.reshape((groups, 2, half) + matrix.shape[1:])
    factor = scales.reshape((groups, 2, half, scales.shape[1]) + (1,) * (matrix.ndim - 2))
    upper = factor[:, 0] * shaped[:, 0]
    lower = factor[:, 1] * shaped[:, 1]
    return (jnp.stack([upper + lower, upper - lower], axis=1) * root_half).reshape(matrix.shape)


def row_butterfly(matrix, seeds):
    scales = seed_values(seeds)
    return row_level(row_level(matrix, scales[0], 1), scales[1], 2)


def col_level(matrix, scales, mover, col_index, span):
    own_part = scales * matrix
    partner = mover(own_part)
    on_top = col_index // span % 2 == 0
    return jnp.where(on_top, own_part + partner, partner - own_part) * root_half


def col_butterfly(matrix, seeds, first_mover, second_mover):
    scales = seed_values(seeds)
    col_count = lax.axis_size("col")
    col_index = lax.axis_index("col")
    blocks_all = matrix.shape[1] * col_count
    span_one = blocks_all // 2
    span_two = blocks_all // 4
    matrix = col_level(matrix, scales[0], first_mover, col_index, span_one)
    return col_level(matrix, scales[1], second_mover, col_index, span_two)


def solve_block(pivot, rows_given):
    gram = jnp.dot(
        pivot.T, pivot, precision=lax.Precision.HIGHEST, preferred_element_type=jnp.float32
    )
    factor = jnp.linalg.cholesky(gram)
    right_side = jnp.dot(
        pivot.T, rows_given, precision=lax.Precision.HIGHEST, preferred_element_type=jnp.float32
    )
    middle = lax.linalg.triangular_solve(factor, right_side, left_side=True, lower=True)
    return lax.linalg.triangular_solve(factor, middle, left_side=True, lower=True, transpose_a=True)


def pivot_pieces(state, step):
    row_blocks = state.shape[0]
    block = state.shape[1]
    col_blocks = state.shape[2]
    row_count = lax.axis_size("row")
    col_count = lax.axis_size("col")
    target = row_blocks * row_count - STEPS + step
    row_root = target % row_count
    row_local = target // row_count
    col_root = target % col_count
    col_local = target // col_count
    on_row = lax.axis_index("row") == row_root
    on_col = lax.axis_index("col") == col_root
    identity = jnp.eye(block, dtype=jnp.float32)
    column = from_root(state[:, :, col_local, :], "col", col_root)
    pivot = jnp.where(on_row, column[row_local], identity)
    left_part = column.at[row_local].set(jnp.where(on_row, pivot - identity, column[row_local]))
    last_column = jnp.where(on_col, 0.0, state[:, :, col_local, :])
    last_column = last_column.at[row_local].set(
        jnp.where(on_row & on_col, identity, last_column[row_local])
    )
    shifted = state.at[:, :, col_local, :].set(last_column)
    pivot_rows = shifted[row_local].reshape(block, col_blocks * block)
    rows_there, pivot_there = (
        broadcast(pivot_rows, "row", row_root),
        broadcast(pivot, "row", row_root),
    )
    right_part = solve_block(pivot_there, rows_there)
    return (shifted, left_part, right_part)


def apply_update(shifted, left_part, right_part):
    row_blocks, block, col_blocks, _ = shifted.shape
    flat_left = left_part.reshape(row_blocks * block, block)
    update = shifted.reshape(row_blocks * block, col_blocks * block) - jnp.dot(
        flat_left, right_part, precision=lax.Precision.HIGHEST, preferred_element_type=jnp.float32
    )
    return update.reshape(shifted.shape)


def per_device(inverse_state, row_seeds, col_seeds):
    row_blocks = inverse_state.shape[0]
    block = inverse_state.shape[1]
    col_blocks = inverse_state.shape[2]
    col_count = lax.axis_size("col")
    state = inverse_state
    shifted, left_part, right_part = pivot_pieces(state, 0)
    state = apply_update(shifted, left_part, right_part)
    shifted, left_part, right_part = pivot_pieces(state, STEPS - 1)
    blocks_all = col_blocks * col_count
    bit_one = (blocks_all // 2).bit_length() - 1
    bit_two = (blocks_all // 4).bit_length() - 1
    moved = row_butterfly(shifted, row_seeds)
    moved = col_butterfly(
        moved.reshape(row_blocks * block, col_blocks, block),
        col_seeds,
        lambda values: swapped(values, "col", bit_one),
        lambda values: swapped(values, "col", bit_two),
    )
    left_moved = row_butterfly(left_part, row_seeds).reshape(row_blocks * block, block)
    right_moved = col_butterfly(
        right_part.reshape(block, col_blocks, block),
        col_seeds,
        lambda values: swapped(values, "col", bit_one),
        lambda values: swapped(values, "col", bit_two),
    )
    product = jnp.dot(
        left_moved,
        right_moved.reshape(block, col_blocks * block),
        precision=lax.Precision.HIGHEST,
        preferred_element_type=jnp.float32,
    )
    result = moved - product.reshape(moved.shape)
    return result.reshape(inverse_state.shape)


def solution(mesh):
    placed = (P(None, "row", None, "col"), P(None, None, "row"), P(None, None, "col"))
    return jax.shard_map(
        per_device,
        mesh=mesh,
        in_specs=placed,
        out_specs=P(None, "row", None, "col"),
        check_vma=False,
    )
```

profile of v0, /device:TPU:2, one launch (start us, length us, event | category | flops | bytes accessed | tf_op | source)
XLA Modules:
  0.0 705.1 jit_solution(6632455285220665631)
XLA Ops:
  6.5 2.4 copy_select_fusion
  9.0 120.5 %reduce-scatter.3.cloned.1.call-done = f32[32,256]{1,0:T(8,128)} async-done(((f32[1024,256]{1,0:T(8,128)}), f32[32,256]{1,0:T(8,128)}) %reduce-scatter.3.cloned.1.call-update) | async-done | bytes 32784 | tf_op jit(solution)/shard_map/reduce_scatter | solution.py:20
  129.6 78.4 %all-gather.9.cloned.1.call-done = f32[1024,256]{1,0:T(8,128)} async-done(((f32[32,256]{1,0:T(8,128)}), f32[1024,256]{1,0:T(8,128)}) %all-gather.9.cloned.1.call-update) | async-done | bytes 1048592 | tf_op jit(solution)/shard_map/all_gather | solution.py:21
  208.0 1.8 convert_select_fusion.1
  209.9 0.7 convert_select_fusion.3
  210.9 49.9 %all-gather.17.cloned.1.call-done = f32[2048,256]{1,0:T(8,128)} async-done(((f32[256,256]{1,0:T(8,128)}), f32[2048,256]{1,0:T(8,128)}) %all-gather.17.cloned.1.call-update) | async-done | bytes 2097168 | tf_op jit(solution)/shard_map/all_gather | solution.py:25
  260.8 1.6 fusion.30
  262.6 11.7 %cholesky.130 = f32[128,128]{1,0:T(8,128)S(1)} custom-call(f32[128,128]{1,0:T(8,128)S(1)} %cholesky.194), custom_call_target="Cholesky" | custom-call | tf_op jit(solution)/shard_map/jit(cholesky)/cholesky | solution.py:79
  274.3 9.8 %custom-call.17 = f32[1,128,128]{1,2,0:T(8,128)S(1)} custom-call(f32[1,128,128]{2,1,0:T(8,128)S(1)} %get-tuple-element.151), custom_call_target="InvertDiagBlocksLowerTriangular" | custom-call | tf_op jit(solution)/shard_map/jit(cholesky)/cholesky | solution.py:79
  284.7 11.7 %cholesky.147 = f32[128,128]{1,0:T(8,128)S(1)} custom-call(f32[128,128]{1,0:T(8,128)S(1)} %convolution_subtract_fusion.6), custom_call_target="Cholesky" | custom-call | tf_op jit(solution)/shard_map/jit(cholesky)/cholesky | solution.py:79
  296.4 0.7 compare_reduce_fusion.2
  298.4 4.3 while.14
  298.9 0.6 fusion.80
  299.5 1.3 bitcast_dynamic-update-slice_fusion.4
  300.8 0.6 fusion.80
  301.4 1.3 bitcast_dynamic-update-slice_fusion.4
  302.8 0.6 copy-done.7
  303.3 19.7 %custom-call.19 = f32[2,128,128]{1,2,0:T(8,128)S(1)} custom-call(f32[2,128,128]{2,1,0:T(8,128)S(1)} %get-tuple-element.109), custom_call_target="InvertDiagBlocksLowerTriangular" | custom-call | tf_op jit(solution)/shard_map/triangular_solve/custom-call.4 | solution.py:84
  323.0 1.6 fusion.13
  326.4 2.0 broadcast_select_fusion
  328.5 116.3 %reduce-scatter.5.cloned.1.call-done = f32[32,256]{1,0:T(8,128)} async-done(((f32[1024,256]{1,0:T(8,128)}), f32[32,256]{1,0:T(8,128)}) %reduce-scatter.5.cloned.1.call-update) | async-done | bytes 32784 | tf_op jit(solution)/shard_map/reduce_scatter | solution.py:20
  444.8 78.2 %all-gather.13.cloned.1.call-done = f32[1024,256]{1,0:T(8,128)} async-done(((f32[32,256]{1,0:T(8,128)}), f32[1024,256]{1,0:T(8,128)}) %all-gather.13.cloned.1.call-update) | async-done | bytes 1048592 | tf_op jit(solution)/shard_map/all_gather | solution.py:21
  523.1 1.7 convert_select_fusion
  525.7 1.0 bitcast_multiply_fusion
  526.8 1.4 collective-permute-start
  528.2 0.7 convert_select_fusion.2
  529.1 0.6 slice_bitcast_fusion.17
  529.7 42.1 %collective-permute-done = f32[1024,1,256]{2,0,1:T(8,128)S(1)} collective-permute-done((f32[1024,1,256]{2,0,1:T(8,128)}, f32[1024,1,256]{2,0,1:T(8,128)S(1)}, u32[]{:S(2)}, u32[]{:S(2)}) %collective-permute-start) | collective-permute-done | bytes 1048608 | tf_op jit(solution)/shard_map/ppermute | solution.py:35
  571.8 1.0 copy-done.1
  572.8 1.4 select_multiply_fusion
  574.2 0.5 collective-permute-start.1
  574.7 1.2 copy.41
  576.0 1.0 fusion.11
  577.0 16.8 %all-gather.19.cloned.1.call-done = f32[2048,256]{1,0:T(8,128)} async-done(((f32[256,256]{1,0:T(8,128)}), f32[2048,256]{1,0:T(8,128)}) %all-gather.19.cloned.1.call-update) | async-done | bytes 2097168 | tf_op jit(solution)/shard_map/all_gather | solution.py:25
  593.8 1.6 fusion.27
  595.4 0.8 copy.16
  596.2 1.0 fusion.21
  597.2 0.7 copy-done.3
  597.9 11.7 %cholesky.164 = f32[128,128]{1,0:T(8,128)S(1)} custom-call(f32[128,128]{1,0:T(8,128)S(1)} %cholesky.197), custom_call_target="Cholesky" | custom-call | tf_op jit(solution)/shard_map/jit(cholesky)/cholesky | solution.py:79
  609.7 0.6 select_reduce_fusion.1
  610.2 9.8 %custom-call.20 = f32[1,128,128]{1,2,0:T(8,128)S(1)} custom-call(f32[1,128,128]{2,1,0:T(8,128)S(1)} %get-tuple-element.147), custom_call_target="InvertDiagBlocksLowerTriangular" | custom-call | tf_op jit(solution)/shard_map/jit(cholesky)/cholesky | solution.py:79
  620.0 1.0 constant_dynamic-update-slice_fusion
  621.1 1.1 convolution_subtract_fusion.5
  622.2 11.7 %cholesky.181 = f32[128,128]{1,0:T(8,128)S(1)} custom-call(f32[128,128]{1,0:T(8,128)S(1)} %convolution_subtract_fusion.5), custom_call_target="Cholesky" | custom-call | tf_op jit(solution)/shard_map/jit(cholesky)/cholesky | solution.py:79
  634.0 0.6 compare_reduce_fusion
  634.6 1.3 compare_reduce_fusion.1
  637.1 1.0 select_select_fusion
  638.1 5.5 while.15
  638.3 0.7 constant_dynamic-slice_fusion.5
  639.0 0.6 fusion.81
  639.6 1.4 bitcast_dynamic-update-slice_fusion.5
  640.9 0.7 constant_dynamic-slice_fusion.5
  641.6 0.6 fusion.81
  642.2 1.4 bitcast_dynamic-update-slice_fusion.5
  643.6 0.6 copy-done.4
  644.2 20.5 %custom-call.22 = f32[2,128,128]{1,2,0:T(8,128)S(1)} custom-call(f32[2,128,128]{2,1,0:T(8,128)} %copy-done.4), custom_call_target="InvertDiagBlocksLowerTriangular" | custom-call | tf_op jit(solution)/shard_map/triangular_solve/custom-call.4 | solution.py:84
  664.8 1.6 fusion.12
  668.2 1.8 collective-permute-start.2
  669.9 0.9 add_bitcast_fusion
  671.0 7.0 collective-permute-done.2
  678.0 3.3 collective-permute-start.3
  681.6 13.4 %collective-permute-done.3 = f32[256,1,256]{2,0,1:T(8,128)S(1)} collective-permute-done((f32[256,1,256]{2,0,1:T(8,128)S(1)}, f32[256,1,256]{2,0,1:T(8,128)S(1)}, u32[]{:S(2)}, u32[]{:S(2)}) %collective-permute-start.3) | collective-permute-done | bytes 262176 | tf_op jit(solution)/shard_map/ppermute | solution.py:35
  695.0 1.1 multiply_subtract_fusion
  696.0 2.0 copy.17
  (89 shorter events, 6.3 us)
Async XLA Ops:
  6.5 123.0 %reduce-scatter.3.cloned.1.call-start = ((), (), s32[]{:S(2)}) async-start(), calls=%async_computation.2 | async-start | bytes 1081344 | tf_op jit(solution)/shard_map/reduce_scatter | solution.py:20
  9.0 199.1 %all-gather.9.cloned.1.call-start = ((), (), s32[]{:S(2)}) async-start(), calls=%async_computation.3 | async-start | bytes 1081344 | tf_op jit(solution)/shard_map/all_gather | solution.py:21
  129.6 131.2 %all-gather.17.cloned.1.call-start = ((), (), s32[]{:S(2)}) async-start(), calls=%async_computation.8 | async-start | bytes 2359296 | tf_op jit(solution)/shard_map/all_gather | solution.py:25
  208.0 2.7 copy-start
  209.8 113.2 %all-gather.11.cloned.1.call-start = ((), (), s32[]{:S(2)}) async-start(), calls=%async_computation.4 | async-start | bytes 2359296 | tf_op jit(solution)/shard_map/all_gather | solution.py:25
  210.6 234.1 %reduce-scatter.5.cloned.1.call-start = ((), (), s32[]{:S(2)}) async-start(), calls=%async_computation.5 | async-start | bytes 1081344 | tf_op jit(solution)/shard_map/reduce_scatter | solution.py:20
  302.7 0.6 copy-start.7
  326.4 198.4 %copy-start.5 = (s32[2,4,256]{2,1,0:T(4,128)S(1)}, s32[2,4,256]{2,1,0:T(4,128)}, u32[]{:S(2)}) copy-start(s32[2,4,256]{2,1,0:T(4,128)} %param.21) | copy-start | bytes 24580
  326.4 198.5 %copy-start.6 = (s32[2,1,256]{2,1,0:T(1,128)S(1)}, s32[2,1,256]{2,1,0:T(1,128)}, u32[]{:S(2)}) copy-start(s32[2,1,256]{2,1,0:T(1,128)} %param.22) | copy-start | bytes 6148
  328.4 194.7 %all-gather.13.cloned.1.call-start = ((), (), s32[]{:S(2)}) async-start(), calls=%async_computation.6 | async-start | bytes 1081344 | tf_op jit(solution)/shard_map/all_gather | solution.py:21
  444.8 149.0 %all-gather.19.cloned.1.call-start = ((), (), s32[]{:S(2)}) async-start(), calls=%async_computation.9 | async-start | bytes 2359296 | tf_op jit(solution)/shard_map/all_gather | solution.py:25
  524.8 140.0 %all-gather.15.cloned.1.call-start = ((), (), s32[]{:S(2)}) async-start(), calls=%async_computation.7 | async-start | bytes 2359296 | tf_op jit(solution)/shard_map/all_gather | solution.py:25
  526.8 45.0 %collective-permute-start = (f32[1024,1,256]{2,0,1:T(8,128)}, f32[1024,1,256]{2,0,1:T(8,128)S(1)}, u32[]{:S(2)}, u32[]{:S(2)}) collective-permute-start(f32[1024,1,256]{2,0,1:T(8,128)} %bitcast_multiply_fusion), channel_id=1, source_target_pairs={{0,16},{16,0},{1,17},{17,1},{2,18},{18,2},{3,19},{19,3},{4,20},{20... | collective-permute-start | bytes 3145736 | tf_op jit(solution)/shard_map/ppermute | solution.py:35
  571.8 1.0 copy-start.1
  574.2 107.4 %collective-permute-start.1 = (f32[1024,1,256]{2,0,1:T(8,128)S(1)}, f32[1024,1,256]{2,0,1:T(8,128)S(1)}, u32[]{:S(2)}, u32[]{:S(2)}) collective-permute-start(f32[1024,1,256]{2,0,1:T(8,128)S(1)} %select_multiply_fusion), channel_id=1, source_target_pairs={{0,8},{8,0},{1,9},{9,1},{2,10},{10,2},{3,11},{11,3},{4,12},{12,4},... | collective-permute-start | bytes 3145736 | tf_op jit(solution)/shard_map/ppermute | solution.py:35
  597.2 0.7 copy-start.3
  634.0 3.1 copy-start.2
  643.6 0.7 copy-start.4
  668.2 9.7 %collective-permute-start.2 = (f32[256,1,256]{2,0,1:T(8,128)S(1)}, f32[256,1,256]{2,0,1:T(8,128)S(1)}, u32[]{:S(2)}, u32[]{:S(2)}) collective-permute-start(f32[256,1,256]{2,0,1:T(8,128)S(1)} %fusion.17), channel_id=1, source_target_pairs={{0,16},{16,0},{1,17},{17,1},{2,18},{18,2},{3,19},{19,3},{4,20},{20... | collective-permute-start | bytes 786440 | tf_op jit(solution)/shard_map/ppermute | solution.py:35
  678.0 17.0 %collective-permute-start.3 = (f32[256,1,256]{2,0,1:T(8,128)S(1)}, f32[256,1,256]{2,0,1:T(8,128)S(1)}, u32[]{:S(2)}, u32[]{:S(2)}) collective-permute-start(f32[256,1,256]{2,0,1:T(8,128)S(1)} %select_multiply_fusion.1), channel_id=1, source_target_pairs={{0,8},{8,0},{1,9},{9,1},{2,10},{10,2},{3,11},{11,3},{4,12},{12,4},... | collective-permute-start | bytes 786440 | tf_op jit(solution)/shard_map/ppermute | solution.py:35
Sparse Core Ops, SparseCore 0:
  11.4 118.0 reduce-scatter.2
  132.3 75.6 all-gather.8
  209.9 50.7 all-gather.16
  262.4 54.0 all-gather.10
  328.5 116.1 reduce-scatter.4
  447.4 75.6 all-gather.12
  524.9 68.8 all-gather.18
  595.6 50.4 all-gather.14
where the time goes:
time: 714 us; the launch traced here: 705 us
  waiting for transfers between devices  523 us (73%)
  other arithmetic  125 us (18%)
  local copies, waits for them, and re-layouts  17.2 us (2%)
  between operations  16.8 us (2%)
  matrix products  15.6 us (2%)
  starting transfers between devices  7.33 us (1%)
    reduce_scatter x2, waiting for transfers between devices, from_root(): own = lax.psum_scatter(padded, axis, scatter_dimension=0, tiled=True)  237 us
    all_gather x2, waiting for transfers between devices, from_root(): lax.all_gather(own, axis, axis=0, tiled=True)[:len(lines)].reshape(x.shape)  157 us
    another operation x13, other arithmetic, solve_block(): factor = jnp.linalg.cholesky(gram)  69.7 us
    all_gather x4, waiting for transfers between devices, broadcast(): lax.all_gather(x, axis)  66.7 us
    ppermute x4, waiting for transfers between devices, swapped(): return lax.ppermute(block, axis, route)  62.5 us
    another operation x5, other arithmetic, solve_block(): lax.linalg.triangular_solve(factor, middle, left_side=True, lower=True, t...  41.2 us
  transfers between devices with their start and end apart: 12, of which 9 were waited for; matrix products, arithmetic and copies ran while one was open for 20% of the time, Pallas kernels for 0%

commit v1 on v0

--- a/solution.py
+++ b/solution.py
@@ -18,7 +18,10 @@
     )
     padded = filled_up(lines, lax.axis_size(axis))
     own = lax.psum_scatter(padded, axis, scatter_dimension=0, tiled=True)
-    return lax.all_gather(own, axis, axis=0, tiled=True)[: len(lines)].reshape(x.shape)
+    return jnp.concatenate(
+        jax.lax.all_to_all(jnp.stack([own for _ in range(jax.lax.axis_size(axis))]), axis, 0, 0),
+        axis=0,
+    )[: len(lines)].reshape(x.shape)
 
 
 def broadcast(x, axis, root):

time: 714 us -> 623 us (0.87)
  the two profiles are of different devices: /device:TPU:2 before, /device:TPU:36 now
where the time goes in v1:
time: 623 us; the launch traced here: 613 us
  waiting for transfers between devices  428 us (69%)
  other arithmetic  117 us (19%)
  starting transfers between devices  21.7 us (3%)
  between operations  16.9 us (3%)
  matrix products  15.1 us (2%)
  local copies, waits for them, and re-layouts  14.2 us (2%)
    reduce_scatter x2, waiting for transfers between devices, from_root(): own = lax.psum_scatter(padded, axis, scatter_dimension=0, tiled=True)  233 us
    all_gather x4, waiting for transfers between devices, broadcast(): lax.all_gather(x, axis)  73.1 us
    another operation x13, other arithmetic, solve_block(): factor = jnp.linalg.cholesky(gram)  68.6 us
    ppermute x4, waiting for transfers between devices, swapped(): return lax.ppermute(block, axis, route)  65.3 us
    all_to_all x2, waiting for transfers between devices, from_root(): jax.lax.all_to_all(jnp.stack([own for _ in range(jax.lax.axis_size(axis))...  55.9 us
    another operation x5, other arithmetic, solve_block(): lax.linalg.triangular_solve(factor, middle, left_side=True, lower=True, t...  39.4 us
    all_to_all x2, starting transfers between devices, from_root(): jax.lax.all_to_all(jnp.stack([own for _ in range(jax.lax.axis_size(axis))...  16.3 us
  transfers between devices with their start and end apart: 12, of which 9 were waited for; matrix products, arithmetic and copies ran while one was open for 21% of the time, Pallas kernels for 0%

profile of v1, /device:TPU:36, one launch (start us, length us, event | category | flops | bytes accessed | tf_op | source)
XLA Modules:
  0.0 613.4 jit_solution(17442196088689440005)
XLA Ops:
  6.5 2.4 copy_select_fusion
  9.0 119.3 %reduce-scatter.3.cloned.1.call-done = f32[32,256]{1,0:T(8,128)} async-done(((f32[1024,256]{1,0:T(8,128)}), f32[32,256]{1,0:T(8,128)}) %reduce-scatter.3.cloned.1.call-update) | async-done | bytes 32784 | tf_op jit(solution)/shard_map/reduce_scatter | solution.py:20
  128.2 1.8 stack.22
  130.1 8.1 %all-to-all-start = ((f32[32,32,256]{2,1,0:T(8,128)}), f32[32,32,256]{2,1,0:T(8,128)S(1)}, u32[]{:S(2)}, u32[]{:S(2)}) async-start(f32[32,32,256]{2,1,0:T(8,128)} %stack.22), calls=%async_computation.1 | async-start | bytes 2097152 | tf_op jit(solution)/shard_map/all_to_all | solution.py:22
  138.2 27.9 %all-to-all-done = f32[32,32,256]{2,1,0:T(8,128)S(1)} async-done(((f32[32,32,256]{2,1,0:T(8,128)}), f32[32,32,256]{2,1,0:T(8,128)S(1)}, u32[]{:S(2)}, u32[]{:S(2)}) %all-to-all-start) | async-done | bytes 1048608 | tf_op jit(solution)/shard_map/all_to_all | solution.py:22
  166.2 0.7 convert_select_fusion.3
  167.0 0.7 convert_select_fusion.2
  167.9 51.6 %all-gather.5.cloned.1.call-done = f32[8,256,256]{2,1,0:T(8,128)} async-done(((f32[1,256,256]{2,1,0:T(8,128)}), f32[8,256,256]{2,1,0:T(8,128)}) %all-gather.5.cloned.1.call-update) | async-done | bytes 2097168 | tf_op jit(solution)/shard_map/all_gather | solution.py:28
  219.5 1.6 fusion.25
  221.3 11.7 %cholesky.130 = f32[128,128]{1,0:T(8,128)S(1)} custom-call(f32[128,128]{1,0:T(8,128)S(1)} %cholesky.194), custom_call_target="Cholesky" | custom-call | tf_op jit(solution)/shard_map/jit(cholesky)/cholesky | solution.py:82
  233.1 9.8 %custom-call.17 = f32[1,128,128]{1,2,0:T(8,128)S(1)} custom-call(f32[1,128,128]{2,1,0:T(8,128)S(1)} %get-tuple-element.155), custom_call_target="InvertDiagBlocksLowerTriangular" | custom-call | tf_op jit(solution)/shard_map/jit(cholesky)/cholesky | solution.py:82
  243.1 0.3 convolution_subtract_fusion.6
  243.4 11.7 %cholesky.147 = f32[128,128]{1,0:T(8,128)S(1)} custom-call(f32[128,128]{1,0:T(8,128)S(1)} %convolution_subtract_fusion.6), custom_call_target="Cholesky" | custom-call | tf_op jit(solution)/shard_map/jit(cholesky)/cholesky | solution.py:82
  255.1 0.7 compare_reduce_fusion.2
  257.3 4.5 while.14
  257.8 0.6 fusion.74
  258.4 1.4 bitcast_dynamic-update-slice_fusion.4
  259.8 0.6 fusion.74
  260.4 1.4 bitcast_dynamic-update-slice_fusion.4
  261.8 19.7 %custom-call.19 = f32[2,128,128]{1,2,0:T(8,128)S(1)} custom-call(f32[2,128,128]{2,1,0:T(8,128)S(1)} %get-tuple-element.109), custom_call_target="InvertDiagBlocksLowerTriangular" | custom-call | tf_op jit(solution)/shard_map/triangular_solve/custom-call.4 | solution.py:87
  281.5 1.6 fusion.11
  283.2 0.3 fusion.29
  283.5 0.3 convolution_subtract_fusion.4
  283.8 0.3 fusion.40
  284.1 0.3 fusion.41
  284.3 0.3 convolution_subtract_fusion.3
  284.7 0.3 fusion.39
  284.9 2.0 broadcast_select_fusion
  286.9 113.9 %reduce-scatter.5.cloned.1.call-done = f32[32,256]{1,0:T(8,128)} async-done(((f32[1024,256]{1,0:T(8,128)}), f32[32,256]{1,0:T(8,128)}) %reduce-scatter.5.cloned.1.call-update) | async-done | bytes 32784 | tf_op jit(solution)/shard_map/reduce_scatter | solution.py:20
  400.8 1.8 stack.28
  402.7 8.2 %all-to-all-start.1 = ((f32[32,32,256]{2,1,0:T(8,128)}), f32[32,32,256]{2,1,0:T(8,128)S(1)}, u32[]{:S(2)}, u32[]{:S(2)}) async-start(f32[32,32,256]{2,1,0:T(8,128)} %stack.28), calls=%async_computation.3 | async-start | bytes 2097152 | tf_op jit(solution)/shard_map/all_to_all | solution.py:22
  411.0 27.9 %all-to-all-done.1 = f32[32,32,256]{2,1,0:T(8,128)S(1)} async-done(((f32[32,32,256]{2,1,0:T(8,128)}), f32[32,32,256]{2,1,0:T(8,128)S(1)}, u32[]{:S(2)}, u32[]{:S(2)}) %all-to-all-start.1) | async-done | bytes 1048608 | tf_op jit(solution)/shard_map/all_to_all | solution.py:22
  438.9 0.7 convert_select_fusion.1
  440.6 1.0 bitcast_multiply_fusion
  441.7 3.0 collective-permute-start
  444.7 0.7 convert_select_fusion
  445.6 41.2 %collective-permute-done = f32[1024,1,256]{2,0,1:T(8,128)} collective-permute-done((f32[1024,1,256]{2,0,1:T(8,128)}, f32[1024,1,256]{2,0,1:T(8,128)}, u32[]{:S(2)}, u32[]{:S(2)}) %collective-permute-start) | collective-permute-done | bytes 1048608 | tf_op jit(solution)/shard_map/ppermute | solution.py:38
  486.8 1.4 select_multiply_fusion
  488.2 0.3 collective-permute-start.1
  488.5 21.5 %all-gather.9.cloned.1.call-done = f32[8,256,256]{2,1,0:T(8,128)} async-done(((f32[1,256,256]{2,1,0:T(8,128)}), f32[8,256,256]{2,1,0:T(8,128)}) %all-gather.9.cloned.1.call-update) | async-done | bytes 2097168 | tf_op jit(solution)/shard_map/all_gather | solution.py:28
  510.0 1.6 fusion.26
  511.8 11.7 %cholesky.164 = f32[128,128]{1,0:T(8,128)S(1)} custom-call(f32[128,128]{1,0:T(8,128)S(1)} %cholesky.197), custom_call_target="Cholesky" | custom-call | tf_op jit(solution)/shard_map/jit(cholesky)/cholesky | solution.py:82
  523.5 9.8 %custom-call.20 = f32[1,128,128]{1,2,0:T(8,128)S(1)} custom-call(f32[1,128,128]{2,1,0:T(8,128)S(1)} %get-tuple-element.151), custom_call_target="InvertDiagBlocksLowerTriangular" | custom-call | tf_op jit(solution)/shard_map/jit(cholesky)/cholesky | solution.py:82
  533.6 0.3 convolution_subtract_fusion.5
  533.9 11.7 %cholesky.181 = f32[128,128]{1,0:T(8,128)S(1)} custom-call(f32[128,128]{1,0:T(8,128)S(1)} %convolution_subtract_fusion.5), custom_call_target="Cholesky" | custom-call | tf_op jit(solution)/shard_map/jit(cholesky)/cholesky | solution.py:82
  545.6 0.6 compare_reduce_fusion.1
  546.3 0.6 compare_reduce_fusion
  548.2 4.1 while.15
  548.4 0.6 fusion.75
  549.0 1.3 bitcast_dynamic-update-slice_fusion.5
  550.4 0.6 fusion.75
  550.9 1.3 bitcast_dynamic-update-slice_fusion.5
  552.3 19.7 %custom-call.22 = f32[2,128,128]{1,2,0:T(8,128)S(1)} custom-call(f32[2,128,128]{2,1,0:T(8,128)S(1)} %get-tuple-element.111), custom_call_target="InvertDiagBlocksLowerTriangular" | custom-call | tf_op jit(solution)/shard_map/triangular_solve/custom-call.4 | solution.py:87
  572.0 1.6 fusion.10
  573.6 0.3 fusion.27
  573.9 0.3 convolution_subtract_fusion.2
  574.2 0.3 fusion.43
  574.5 0.3 fusion.44
  574.8 0.3 convolution_subtract_fusion.1
  575.8 9.3 %collective-permute-done.2 = f32[256,1,256]{2,0,1:T(8,128)S(1)} collective-permute-done((f32[256,1,256]{2,0,1:T(8,128)S(1)}, f32[256,1,256]{2,0,1:T(8,128)S(1)}, u32[]{:S(2)}, u32[]{:S(2)}) %collective-permute-start.2) | collective-permute-done | bytes 262176 | tf_op jit(solution)/shard_map/ppermute | solution.py:38
  585.1 1.8 collective-permute-start.3
  587.3 14.8 %collective-permute-done.3 = f32[256,1,256]{2,0,1:T(8,128)S(1)} collective-permute-done((f32[256,1,256]{2,0,1:T(8,128)S(1)}, f32[256,1,256]{2,0,1:T(8,128)S(1)}, u32[]{:S(2)}, u32[]{:S(2)}) %collective-permute-start.3) | collective-permute-done | bytes 262176 | tf_op jit(solution)/shard_map/ppermute | solution.py:38
  602.0 2.3 multiply_subtract_fusion
  604.3 2.0 copy.17
  (75 shorter events, 3.4 us)
Async XLA Ops:
  6.5 121.7 %reduce-scatter.3.cloned.1.call-start = ((), (), s32[]{:S(2)}) async-start(), calls=%async_computation.4 | async-start | bytes 1081344 | tf_op jit(solution)/shard_map/reduce_scatter | solution.py:20
  130.1 36.1 %all-to-all-start = ((f32[32,32,256]{2,1,0:T(8,128)}), f32[32,32,256]{2,1,0:T(8,128)S(1)}, u32[]{:S(2)}, u32[]{:S(2)}) async-start(f32[32,32,256]{2,1,0:T(8,128)} %stack.22), calls=%async_computation.1 | async-start | bytes 2097152 | tf_op jit(solution)/shard_map/all_to_all | solution.py:22
  138.2 81.3 %all-gather.5.cloned.1.call-start = ((), (), s32[]{:S(2)}) async-start(), calls=%async_computation.5 | async-start | bytes 2359296 | tf_op jit(solution)/shard_map/all_gather | solution.py:28
  167.0 114.6 %all-gather.7.cloned.1.call-start = ((), (), s32[]{:S(2)}) async-start(), calls=%async_computation.6 | async-start | bytes 2359296 | tf_op jit(solution)/shard_map/all_gather | solution.py:28
  167.8 233.0 %reduce-scatter.5.cloned.1.call-start = ((), (), s32[]{:S(2)}) async-start(), calls=%async_computation.7 | async-start | bytes 1081344 | tf_op jit(solution)/shard_map/reduce_scatter | solution.py:20
  402.7 37.1 %copy-start = (s32[2,4,256]{2,1,0:T(4,128)S(1)}, s32[2,4,256]{2,1,0:T(4,128)}, u32[]{:S(2)}) copy-start(s32[2,4,256]{2,1,0:T(4,128)} %param.21) | copy-start | bytes 24580
  402.7 37.1 %copy-start.1 = (s32[2,1,256]{2,1,0:T(1,128)S(1)}, s32[2,1,256]{2,1,0:T(1,128)}, u32[]{:S(2)}) copy-start(s32[2,1,256]{2,1,0:T(1,128)} %param.22) | copy-start | bytes 6148
  402.7 36.2 %all-to-all-start.1 = ((f32[32,32,256]{2,1,0:T(8,128)}), f32[32,32,256]{2,1,0:T(8,128)S(1)}, u32[]{:S(2)}, u32[]{:S(2)}) async-start(f32[32,32,256]{2,1,0:T(8,128)} %stack.28), calls=%async_computation.3 | async-start | bytes 2097152 | tf_op jit(solution)/shard_map/all_to_all | solution.py:22
  410.9 99.1 %all-gather.9.cloned.1.call-start = ((), (), s32[]{:S(2)}) async-start(), calls=%async_computation.8 | async-start | bytes 2359296 | tf_op jit(solution)/shard_map/all_gather | solution.py:28
  439.7 132.3 %all-gather.11.cloned.1.call-start = ((), (), s32[]{:S(2)}) async-start(), calls=%async_computation.9 | async-start | bytes 2359296 | tf_op jit(solution)/shard_map/all_gather | solution.py:28
  441.7 45.2 %collective-permute-start = (f32[1024,1,256]{2,0,1:T(8,128)}, f32[1024,1,256]{2,0,1:T(8,128)}, u32[]{:S(2)}, u32[]{:S(2)}) collective-permute-start(f32[1024,1,256]{2,0,1:T(8,128)} %bitcast_multiply_fusion), channel_id=1, source_target_pairs={{0,16},{16,0},{1,17},{17,1},{2,18},{18,2},{3,19},{19,3},{4,20},{20... | collective-permute-start | bytes 3145736 | tf_op jit(solution)/shard_map/ppermute | solution.py:38
  488.2 99.0 %collective-permute-start.1 = (f32[1024,1,256]{2,0,1:T(8,128)S(1)}, f32[1024,1,256]{2,0,1:T(8,128)}, u32[]{:S(2)}, u32[]{:S(2)}) collective-permute-start(f32[1024,1,256]{2,0,1:T(8,128)S(1)} %select_multiply_fusion), channel_id=1, source_target_pairs={{0,8},{8,0},{1,9},{9,1},{2,10},{10,2},{3,11},{11,3},{4,12},{12,4},... | collective-permute-start | bytes 3145736 | tf_op jit(solution)/shard_map/ppermute | solution.py:38
  575.4 9.7 %collective-permute-start.2 = (f32[256,1,256]{2,0,1:T(8,128)S(1)}, f32[256,1,256]{2,0,1:T(8,128)S(1)}, u32[]{:S(2)}, u32[]{:S(2)}) collective-permute-start(f32[256,1,256]{2,0,1:T(8,128)S(1)} %fusion.15), channel_id=1, source_target_pairs={{0,16},{16,0},{1,17},{17,1},{2,18},{18,2},{3,19},{19,3},{4,20},{20... | collective-permute-start | bytes 786440 | tf_op jit(solution)/shard_map/ppermute | solution.py:38
  585.1 16.9 %collective-permute-start.3 = (f32[256,1,256]{2,0,1:T(8,128)S(1)}, f32[256,1,256]{2,0,1:T(8,128)S(1)}, u32[]{:S(2)}, u32[]{:S(2)}) collective-permute-start(f32[256,1,256]{2,0,1:T(8,128)S(1)} %select_multiply_fusion.1), channel_id=1, source_target_pairs={{0,8},{8,0},{1,9},{9,1},{2,10},{10,2},{3,11},{11,3},{4,12},{12,4},... | collective-permute-start | bytes 786440 | tf_op jit(solution)/shard_map/ppermute | solution.py:38
Sparse Core Ops, SparseCore 0:
  11.4 116.7 reduce-scatter.2
  167.1 52.3 all-gather.4
  221.3 54.0 all-gather.6
  287.0 113.7 reduce-scatter.4
  439.8 70.1 all-gather.8
  511.6 50.8 all-gather.10
